TPU v7x, 32 devices: a whole 2x2x4 slice. The times are simulated.
32 devices in a mesh: dp: 8 (over z, x), mp: 4 (over y, core).
Axes of the slice: x: 2, y: 2, z: 4, core: 2. Of those that a mesh axis runs over, the one named last changes fastest.
Arguments:
- hidden_activation: bfloat16 [2, 8, 2, 256, 14336], P(None, 'dp', None, None, 'mp'), may hold values from -6 to 6
- target_head_rows: bfloat16 [2, 8, 2, 256, 4096], P(None, 'dp', None, None, 'mp'), may hold values from -6 to 6
- reference_log_probability: float32 [2, 8, 2, 256], P(None, 'dp'), may hold values from -8 to -0.05
- response_token_mask: int32 [2, 8, 2, 256], P(None, 'dp'), may hold values 0 or 1
- sequence_tile_lengths: int32 [2, 8, 2], P(None, 'dp'), may hold values from 1 to 2
- pair_destination: int32 [2, 8], replicated, may hold values from 0 to 7, each once within a row
- adapter_down_first: bfloat16 [14336, 256], P('mp'), may hold values from -0.046875 to 0.046875
- adapter_down_second: bfloat16 [4096, 256], P('mp'), may hold values from -0.09375 to 0.09375
Outputs:
- pair_margin: float32 [2, 8], P(None, 'dp')
- mean_loss: float32 [], replicated
- grad_a: float32 [14336, 256], P(('mp', 'dp'))
- grad_b: float32 [4096, 256], P(('mp', 'dp'))
Inputs may be any that keep to these rules, and one draw needn't show every extreme that they name: Each row of pair_destination is a permutation of 0 to 7.
All inputs are finite; a program needn't handle non-finite values. No bound on the sum of `response_token_mask` on one device may be relied on, other than what follows from the above.
Results may differ from a plain program's by a relative error of at most 0.0029.
Values sent between devices are 32-bit elements; how exact they have to be, the bound alone decides.
A program may use at most 128 MiB of HBM per device.

v0:
```python
import math

import jax
import jax.numpy as jnp
from jax import lax
from jax.sharding import PartitionSpec as P

MODEL_WIDTH = 4096
HIDDEN_UNITS = 14336
TILE = 128


BETA = 0.1


def per_device(
    hidden_activation,
    target_head_rows,
    reference_log_probability,
    response_token_mask,
    sequence_tile_lengths,
    pair_destination,
    adapter_down_first,
    adapter_down_second,
):
    micro_count, pairs_dev, _, seq_len, ff_dev = hidden_activation.shape
    d_dev = target_head_rows.shape[-1]
    adapter_rank_count = adapter_down_first.shape[1]
    rank_square_root = math.sqrt(adapter_rank_count)
    positions = jnp.arange(seq_len) // TILE
    signs = jnp.array([1.0, -1.0], jnp.float32)
    contract = (((0,), (0,)), ((), ()))
    margin_list = []
    shard_a = None
    shard_b = None
    latent_parts = jnp.stack(
        [
            jnp.dot(
                hidden_activation[step].reshape(-1, ff_dev),
                adapter_down_first,
                preferred_element_type=jnp.float32,
            )
            for step in range(micro_count)
        ]
    )
    readout_parts = jnp.stack(
        [
            jnp.dot(
                target_head_rows[step].reshape(-1, d_dev),
                adapter_down_second,
                preferred_element_type=jnp.float32,
            )
            for step in range(micro_count)
        ]
    )
    summed_latent, summed_readout = lax.psum((latent_parts, readout_parts), "mp")
    for micro_step in range(micro_count):
        hidden_flattened = hidden_activation[micro_step].reshape(-1, ff_dev)
        rows_flattened = target_head_rows[micro_step].reshape(-1, d_dev)
        lengths_now = sequence_tile_lengths[micro_step]
        latent = summed_latent[micro_step]
        readout = summed_readout[micro_step]
        ref_now = reference_log_probability[micro_step]
        shift = (jnp.sum(latent * readout, axis=-1) / rank_square_root).reshape(ref_now.shape)
        chance = jnp.exp(ref_now)
        denom = 1.0 - chance + chance * jnp.exp(shift)
        gain = shift - jnp.log(denom)
        live_mask = (
            (response_token_mask[micro_step] == 1)
            & (positions[None, None, :] < lengths_now[:, :, None])
        ).astype(jnp.float32)
        seq_sums = jnp.sum(live_mask * gain, axis=-1)
        reward_margin = BETA * (seq_sums[:, 0] - seq_sums[:, 1])
        margin_list.append(reward_margin)
        slope = -jax.nn.sigmoid(-reward_margin)
        factor = (
            live_mask
            * (slope * BETA)[:, None, None]
            * signs[None, :, None]
            * (1.0 - chance)
            / denom
            / rank_square_root
        )
        factor = factor.reshape(-1, 1)
        d_latent = (factor * readout).astype(jnp.bfloat16)
        d_readout = (factor * latent).astype(jnp.bfloat16)
        first_portion = lax.dot_general(
            hidden_flattened, d_latent, contract, preferred_element_type=jnp.float32
        )
        second_portion = lax.dot_general(
            rows_flattened, d_readout, contract, preferred_element_type=jnp.float32
        )
        piece_a, piece_b = (
            lax.psum_scatter(first_portion, "dp", scatter_dimension=0, tiled=True),
            lax.psum_scatter(second_portion, "dp", scatter_dimension=0, tiled=True),
        )
        if shard_a is None:
            shard_a, shard_b = (piece_a, piece_b)
        else:
            shard_a = shard_a + piece_a
            shard_b = shard_b + piece_b
    margins = jnp.stack(margin_list)
    all_margins = lax.all_gather(margins, "dp", axis=1, tiled=True)
    place_start = lax.axis_index("dp") * pairs_dev
    targets = place_start + jnp.arange(pairs_dev)
    hits = pair_destination[:, :, None] == targets[None, None, :]
    pair_margin = jnp.sum(jnp.where(hits, all_margins[:, :, None], 0.0), axis=1)
    loss_sum = lax.psum(jnp.sum(jax.nn.softplus(-margins)), "dp")
    mean_loss = loss_sum / (micro_count * pairs_dev * lax.axis_size("dp"))
    squared_values = lax.psum(jnp.sum(shard_a * shard_a) + jnp.sum(shard_b * shard_b), ("dp", "mp"))
    adapter_scale = 1.0 / jnp.sqrt(
        squared_values / (HIDDEN_UNITS * adapter_rank_count + MODEL_WIDTH * adapter_rank_count)
        + 1e-06
    )
    return (pair_margin, mean_loss, shard_a * adapter_scale, shard_b * adapter_scale)


def solution(mesh):
    in_specs = (
        P(None, "dp", None, None, "mp"),
        P(None, "dp", None, None, "mp"),
        P(None, "dp", None, None),
        P(None, "dp", None, None),
        P(None, "dp", None),
        P(),
        P("mp", None),
        P("mp", None),
    )
    out_specs = (P(None, "dp"), P(), P(("mp", "dp"), None), P(("mp", "dp"), None))
    return jax.shard_map(
        per_device, mesh=mesh, in_specs=in_specs, out_specs=out_specs, check_vma=False
    )
```

profile of v0, /device:TPU:0, one launch (start us, length us, event | category | flops | bytes accessed | tf_op | source)
XLA Modules:
  0.0 287.7 jit_solution(17077414794893097699)
XLA Ops:
  7.2 3.7 %fusion.33 = (bf16[1,1,2,256,3584]{4,3,2,1,0:T(8,128)(2,1)S(1)}, bf16[1,1,2,256,3584]{4,3,2,1,0:T(8,128)(2,1)S(1)}) fusion(bf16[2,1,2,256,3584]{4,3,2,1,0:T(8,128)(2,1)} %param.9), kind=kLoop, calls=%fused_computation.71 | loop fusion | bytes 14680064 | tf_op jit(solution)/shard_map/slice | solution.py:39
  11.0 1.1 convolution_bitcast_fusion.2
  12.1 1.1 convolution_bitcast_fusion.3
  13.3 0.8 copy-done.2
  14.1 1.0 copy-done.6
  15.3 0.9 copy-done.7
  16.2 0.5 convolution_bitcast_fusion
  16.6 0.4 convolution_bitcast_fusion.1
  17.1 1.5 pad_maximum_fusion
  18.8 54.1 %all-reduce.3.cloned.1.call-done = (f32[2,512,256]{2,1,0:T(8,128)}, f32[2,512,256]{2,1,0:T(8,128)}) async-done(((f32[2,512,256]{2,1,0:T(8,128)}, f32[2,512,256]{2,1,0:T(8,128)}), (f32[2,512,256]{2,1,0:T(8,128)}, f32[2,512,256]{2,1,0:T(8,128)})) %all-reduce.3.cloned.1.call-update) | async-done | bytes 2097168 | tf_op jit(solution)/shard_map/psum | solution.py:56
  72.9 1.7 multiply_reduce_fusion.2
  74.7 0.2 fusion.24
  74.9 0.6 fusion.35
  76.9 0.6 fusion.36
  79.1 2.0 fusion.8
  81.1 2.6 fusion.1
  83.7 3.6 %fusion.3 = f32[256,3584]{1,0:T(8,128)S(1)} fusion(bf16[512,3584]{1,0:T(8,128)(2,1)} %bitcast.110, f32[2,512,256]{2,1,0:T(8,128)} %get-tuple-element.20, f32[512]{0:T(512)S(1)} %get-tuple-element.29), kind=kOutput, calls=%fused_computation.18 | convolution fusion | flops 939786240 | bytes 7866368 | tf_op jit(solution)/shard_map/dot_general | solution.py:87
  87.3 3.1 %fusion = f32[3584,256]{0,1:T(8,128)} fusion(f32[256,3584]{1,0:T(8,128)S(1)} %fusion.3, bf16[512,3584]{1,0:T(8,128)(2,1)S(1)} %bitcast.112, f32[2,512,256]{2,1,0:T(8,128)S(1)} %copy-done.5, f32[512]{0:T(512)S(1)} %get-tuple-element.28), kind=kOutput, calls=%fused_computation.1 | convolution fusion | flops 940703744 | bytes 11536384 | tf_op jit(solution)/shard_map/dot_general | solution.py:87
  90.5 5.2 %copy.22 = f32[3584,256]{1,0:T(8,128)} copy(f32[3584,256]{0,1:T(8,128)} %fusion) | data formatting | bytes 7340032
  95.7 0.6 fusion.31
  96.3 22.2 %psum.30 = f32[]{:T(128)} all-reduce(f32[]{:T(128)} %fusion.31), channel_id=1, replica_groups=mesh['dp'=8,'mp'=4] {'dp'}, use_global_device_ids=true, to_apply=%region_8.9 | all-reduce | flops 1 | bytes 8 | tf_op jit(solution)/shard_map/psum | solution.py:108
  118.6 16.3 %all-gather = f32[8,1,2]{2,1,0:T(1,128)S(1)} all-gather(f32[1,1,2]{2,1,0:T(1,128)S(1)} %bitcast.125), channel_id=1, replica_groups=mesh['dp'=8,'mp'=4] {'dp'}, dimensions={0}, use_global_device_ids=true | all-gather | bytes 72 | tf_op jit(solution)/shard_map/all_gather | solution.py:103
  135.0 0.6 fusion.30
  135.6 13.0 %reduce-scatter.5.cloned.1.call-done = f32[128,256]{0,1:T(8,128)} async-done(((f32[1024,256]{0,1:T(8,128)}), f32[128,256]{0,1:T(8,128)}) %reduce-scatter.5.cloned.1.call-update) | async-done | bytes 131088 | tf_op jit(solution)/shard_map/reduce_scatter | solution.py:95
  148.6 1.5 multiply_reduce_fusion.3
  150.1 82.4 %reduce-scatter.7.cloned.1.call-done = f32[448,256]{1,0:T(8,128)} async-done(((f32[3584,256]{1,0:T(8,128)}), f32[448,256]{1,0:T(8,128)}) %reduce-scatter.7.cloned.1.call-update) | async-done | bytes 458768
  232.6 1.2 copy.23
  233.8 0.7 multiply_reduce_fusion
  236.5 40.2 %psum.31 = f32[]{:T(128)} all-reduce(f32[]{:T(128)S(6)} %add.104), channel_id=1, replica_groups=mesh['dp'=8,'mp'=4] {'dp','mp'}, use_global_device_ids=true, to_apply=%region_15.16 | all-reduce | flops 1 | bytes 8 | tf_op jit(solution)/shard_map/psum | solution.py:110
  277.5 0.9 broadcast_multiply_fusion.1
  278.4 0.8 copy.21
  279.1 1.0 copy.20
  (50 shorter events, 1.0 us)
Async XLA Ops:
  7.2 3.8 %copy-start = (bf16[3584,256]{1,0:T(8,128)(2,1)S(1)}, bf16[3584,256]{1,0:T(8,128)(2,1)}, u32[]{:S(2)}) copy-start(bf16[3584,256]{1,0:T(8,128)(2,1)} %param.15) | copy-start | bytes 5505028
  7.2 65.7 %all-reduce.3.cloned.1.call-start = ((), (), s32[]{:S(2)}) async-start(), calls=%async_computation.4 | async-start | bytes 4194304 | tf_op jit(solution)/shard_map/psum | solution.py:56
  11.0 2.3 copy-start.1
  11.0 3.1 %copy-start.2 = (bf16[1,1,2,256,3584]{4,3,2,1,0:T(8,128)(2,1)}, bf16[1,1,2,256,3584]{4,3,2,1,0:T(8,128)(2,1)S(1)}, u32[]{:S(2)}) copy-start(bf16[1,1,2,256,3584]{4,3,2,1,0:T(8,128)(2,1)S(1)} %get-tuple-element.25) | copy-start | bytes 11010052
  12.1 3.0 %copy-start.6 = (bf16[2,1,2,256,1024]{4,3,2,1,0:T(8,128)(2,1)S(1)}, bf16[2,1,2,256,1024]{4,3,2,1,0:T(8,128)(2,1)}, u32[]{:S(2)}) copy-start(bf16[2,1,2,256,1024]{4,3,2,1,0:T(8,128)(2,1)} %param.10) | copy-start | bytes 6291460
  15.1 1.0 copy-start.7
  15.3 3.3 %copy-start.4 = (bf16[1,1,2,256,1024]{4,3,2,1,0:T(8,128)(2,1)}, bf16[1,1,2,256,1024]{4,3,2,1,0:T(8,128)(2,1)S(1)}, u32[]{:S(2)}) copy-start(bf16[1,1,2,256,1024]{4,3,2,1,0:T(8,128)(2,1)S(1)} %get-tuple-element.26) | copy-start | bytes 3145732
  17.1 1.6 copy-start.8
  17.1 1.7 copy-start.11
  17.1 57.6 %copy-start.9 = (s32[2,1,2,256]{3,2,1,0:T(2,128)S(1)}, s32[2,1,2,256]{3,2,1,0:T(2,128)}, u32[]{:S(2)}) copy-start(s32[2,1,2,256]{3,2,1,0:T(2,128)} %param.12) | copy-start | bytes 12292
  17.1 61.9 %copy-start.12 = (f32[2]{0:T(128)S(1)}, f32[2]{0:T(128)}, u32[]{:S(2)}) copy-start(f32[2]{0:T(128)} %constant.62.clone) | copy-start | bytes 28
  18.6 130.0 %reduce-scatter.5.cloned.1.call-start = ((), (), s32[]{:S(2)}) async-start(), calls=%async_computation.2 | async-start | bytes 1179648 | tf_op jit(solution)/shard_map/reduce_scatter | solution.py:95
  83.7 3.7 %copy-start.5 = (f32[2,512,256]{2,1,0:T(8,128)S(1)}, f32[2,512,256]{2,1,0:T(8,128)}, u32[]{:S(2)}) copy-start(f32[2,512,256]{2,1,0:T(8,128)} %get-tuple-element.20) | copy-start | bytes 3145732
  83.7 148.9 %reduce-scatter.7.cloned.1.call-start = ((), (), s32[]{:S(2)}) async-start(), calls=%async_computation.3 | async-start | bytes 4128768
  83.7 3.6 %copy-start.3 = (bf16[1,1,2,256,3584]{4,3,2,1,0:T(8,128)(2,1)S(1)}, bf16[1,1,2,256,3584]{4,3,2,1,0:T(8,128)(2,1)}, u32[]{:S(2)}) copy-start(bf16[1,1,2,256,3584]{4,3,2,1,0:T(8,128)(2,1)} %copy-done.2) | copy-start | bytes 11010052
  95.6 39.3 %copy-start.10 = (s32[2,8]{1,0:T(2,128)S(1)}, s32[2,8]{1,0:T(2,128)}, u32[]{:S(2)}) copy-start(s32[2,8]{1,0:T(2,128)} %param.14) | copy-start | bytes 196
Sparse Core Ops, SparseCore 0:
  18.7 54.1 all-reduce.2
  83.8 64.7 reduce-scatter.4
  152.3 80.2 reduce-scatter.6
where the time goes:
time: 288 us
  waiting for transfers between devices  150 us (52%)
  blocking collectives  78.7 us (27%)
  between operations  20.6 us (7%)
  local copies, waits for them, and re-layouts  16.3 us (6%)
  matrix products  14.4 us (5%)
  other arithmetic  8.04 us (3%)
    unnamed x4, waiting for transfers between devices  82.5 us
    psum x1, waiting for transfers between devices, per_device(): lax.psum((latent_parts, readout_parts), 'mp')  54.1 us
    psum x1, blocking collectives, per_device(): lax.psum(jnp.sum(shard_a * shard_a) + jnp.sum(shard_b * shard_b), ('dp',...  40.2 us
    psum x1, blocking collectives, per_device(): loss_sum = lax.psum(jnp.sum(jax.nn.softplus(-margins)), 'dp')  22.2 us
    all_gather x1, blocking collectives, per_device(): all_margins = lax.all_gather(margins, 'dp', axis=1, tiled=True)  16.3 us
    reduce_scatter x1, waiting for transfers between devices, per_device(): lax.psum_scatter(second_portion, 'dp', scatter_dimension=0, tiled=True)  13 us
    unnamed x35, local copies, waits for them, and re-layouts  10.9 us
    dot_general x2, matrix products, per_device(): lax.dot_general(hidden_flattened, d_latent, contract, preferred_element_t...  6.72 us
  transfers between devices with their start and end apart: 3, of which 3 were waited for; matrix products, arithmetic and copies ran while one was open for 5% of the time, Pallas kernels for 0%

commit v1 on v0

v1 whole, which is shorter than its diff:
```python
import math

import jax
import jax.numpy as jnp
from jax import lax
from jax.sharding import PartitionSpec as P

TILE = 128


BETA = 0.1


def per_device(
    hidden_activation,
    target_head_rows,
    reference_log_probability,
    response_token_mask,
    sequence_tile_lengths,
    pair_destination,
    adapter_down_first,
    adapter_down_second,
):
    micro_count, pairs_dev, _, seq_len, ff_dev = hidden_activation.shape
    d_dev = target_head_rows.shape[-1]
    rank = adapter_down_first.shape[1]
    root = math.sqrt(rank)
    dp_size = lax.axis_size("dp")
    positions = jnp.arange(seq_len) // TILE
    signs = jnp.array([1.0, -1.0], jnp.float32)
    contract = (((0,), (0,)), ((), ()))
    hidden = hidden_activation.reshape(-1, ff_dev)
    rows = target_head_rows.reshape(-1, d_dev)
    latent = jnp.dot(hidden, adapter_down_first, preferred_element_type=jnp.float32)
    readout = jnp.dot(rows, adapter_down_second, preferred_element_type=jnp.float32)
    latent, readout = lax.psum((latent, readout), "mp")
    shift = (jnp.sum(latent * readout, axis=-1) / root).reshape(reference_log_probability.shape)
    chance = jnp.exp(reference_log_probability)
    denom = 1.0 - chance + chance * jnp.exp(shift)
    gain = shift - jnp.log(denom)
    live = (
        (response_token_mask == 1) & (positions < sequence_tile_lengths[..., None])
    ).astype(jnp.float32)
    seq_sums = jnp.sum(live * gain, axis=-1)
    margins = BETA * (seq_sums[..., 0] - seq_sums[..., 1])
    slope = -jax.nn.sigmoid(-margins)
    factor = (
        live
        * (slope * BETA)[..., None, None]
        * signs[:, None]
        * (1.0 - chance)
        / denom
        / root
    ).reshape(-1, 1)
    d_latent = (factor * readout).astype(jnp.bfloat16)
    d_readout = (factor * latent).astype(jnp.bfloat16)
    raw_a = lax.dot_general(hidden, d_latent, contract, preferred_element_type=jnp.float32)
    raw_b = lax.dot_general(rows, d_readout, contract, preferred_element_type=jnp.float32)
    shard_a = lax.psum_scatter(raw_a, "dp", scatter_dimension=0, tiled=True)
    shard_b = lax.psum_scatter(raw_b, "dp", scatter_dimension=0, tiled=True)
    all_margins = lax.all_gather(margins, "dp", axis=1, tiled=True)
    targets = lax.axis_index("dp") * pairs_dev + jnp.arange(pairs_dev)
    hits = pair_destination[:, :, None] == targets[None, None, :]
    pair_margin = jnp.sum(jnp.where(hits, all_margins[:, :, None], 0.0), axis=1)
    mean_loss = jnp.mean(jax.nn.softplus(-all_margins))
    squares = lax.psum(jnp.sum(shard_a * shard_a) + jnp.sum(shard_b * shard_b), ("dp", "mp"))
    count = (ff_dev + d_dev) * rank * lax.axis_size("mp")
    scale = 1.0 / jnp.sqrt(squares / count + 1e-06)
    return (pair_margin, mean_loss, shard_a * scale, shard_b * scale)


def solution(mesh):
    in_specs = (
        P(None, "dp", None, None, "mp"),
        P(None, "dp", None, None, "mp"),
        P(None, "dp", None, None),
        P(None, "dp", None, None),
        P(None, "dp", None),
        P(),
        P("mp", None),
        P("mp", None),
    )
    out_specs = (P(None, "dp"), P(), P(("mp", "dp"), None), P(("mp", "dp"), None))
    return jax.shard_map(
        per_device, mesh=mesh, in_specs=in_specs, out_specs=out_specs, check_vma=False
    )
```

time: 288 us -> 279 us (0.969)
  blocking collectives: 78.7 us -> 60.7 us
  waiting for transfers between devices: 150 us -> 168 us
  local copies, waits for them, and re-layouts: 16.3 us -> 8.3 us
  matrix products: 14.4 us -> 18.7 us
  between operations: 20.6 us -> 17.6 us
    psum x1 -> x0, blocking collectives: 22.2 us -> none  [per_device(): loss_sum = lax.psum(jnp.sum(jax.nn.softplus(-margins)), 'dp')]
    reduce_scatter x1, waiting for transfers between devices: 13 us -> 31.2 us  [per_device(): shard_b = lax.psum_scatter(raw_b, 'dp', scatter_dimension=0, tiled=True)]
    slice x4 -> x0, local copies, waits for them, and re-layouts: 5.09 us -> none  [the longest x1 3.74 us: per_device(): hidden_activation[step].reshape(-1, ff_dev)]
    dot_general x8 -> x4, matrix products: 14.4 us -> 18.7 us  [the longest x1 7.1 us: per_device(): lax.dot_general(hidden, d_latent, contract, preferred_element_type=jnp.fl...]
    all_gather x1, blocking collectives: 16.3 us -> 20.5 us  [per_device(): all_margins = lax.all_gather(margins, 'dp', axis=1, tiled=True)]
    unnamed x35 -> x23, local copies, waits for them, and re-layouts: 10.9 us -> 8.11 us
where the time goes in v1:
time: 279 us
  waiting for transfers between devices  168 us (60%)
  blocking collectives  60.7 us (22%)
  matrix products  18.7 us (7%)
  between operations  17.6 us (6%)
  local copies, waits for them, and re-layouts  8.3 us (3%)
  other arithmetic  5.24 us (2%)
    unnamed x4, waiting for transfers between devices  82.4 us
    psum x1, waiting for transfers between devices, per_device(): latent, readout = lax.psum((latent, readout), 'mp')  54.2 us
    psum x1, blocking collectives, per_device(): lax.psum(jnp.sum(shard_a * shard_a) + jnp.sum(shard_b * shard_b), ('dp',...  40.2 us
    reduce_scatter x1, waiting for transfers between devices, per_device(): shard_b = lax.psum_scatter(raw_b, 'dp', scatter_dimension=0, tiled=True)  31.2 us
    all_gather x1, blocking collectives, per_device(): all_margins = lax.all_gather(margins, 'dp', axis=1, tiled=True)  20.5 us
    unnamed x23, local copies, waits for them, and re-layouts  8.11 us
    dot_general x1, matrix products, per_device(): lax.dot_general(hidden, d_latent, contract, preferred_element_type=jnp.fl...  7.1 us
    dot_general x1, matrix products, per_device(): jnp.dot(hidden, adapter_down_first, preferred_element_type=jnp.float32)  6.78 us
  transfers between devices with their start and end apart: 3, of which 3 were waited for; matrix products, arithmetic and copies ran while one was open for 5% of the time, Pallas kernels for 0%

profile of v1, /device:TPU:0, one launch (start us, length us, event | category | flops | bytes accessed | tf_op | source)
XLA Modules:
  0.0 278.5 jit_solution(1153638290707547934)
XLA Ops:
  7.2 0.0 copy-start
  7.2 0.0 all-reduce.3.cloned.1.call-start
  7.2 0.0 copy-start.8
  7.2 6.8 %fusion.4 = f32[1024,256]{1,0:T(8,128)} fusion(bf16[1024,3584]{1,0:T(8,128)(2,1)} %bitcast.26, bf16[3584,256]{1,0:T(8,128)(2,1)} %param.15), kind=kOutput, calls=%fused_computation.28 | convolution fusion | flops 1879048192 | bytes 10223616 | tf_op jit(solution)/shard_map/dot_general | solution.py:34
  14.0 0.0 copy-done
  14.0 1.7 fusion.5
  15.7 0.0 all-reduce.3.cloned.1.call-update
  15.8 0.0 reduce-scatter.5.cloned.1.call-start
  15.8 54.2 %all-reduce.3.cloned.1.call-done = (f32[1024,256]{1,0:T(8,128)}, f32[1024,256]{1,0:T(8,128)}) async-done(((f32[1024,256]{1,0:T(8,128)}, f32[1024,256]{1,0:T(8,128)}), (f32[1024,256]{1,0:T(8,128)}, f32[1024,256]{1,0:T(8,128)})) %all-reduce.3.cloned.1.call-update) | async-done | bytes 2097168 | tf_op jit(solution)/shard_map/psum | solution.py:36
  70.0 1.8 multiply_reduce_fusion
  71.8 0.2 select_reduce_fusion
  72.0 0.2 multiply_reduce_fusion.3
  72.2 0.1 multiply_bitcast_fusion
  72.3 3.1 %convolution_bitcast_fusion.1 = f32[1024,256]{0,1:T(8,128)} fusion(bf16[1024,1024]{1,0:T(8,128)(2,1)S(1)} %bitcast.25, f32[1024,256]{1,0:T(8,128)} %get-tuple-element.18, f32[1024]{0:T(1024)S(1)} %bitcast.28), kind=kOutput, calls=%fused_computation.1 | convolution fusion | flops 537395200 | bytes 4198400 | tf_op jit(solution)/shard_map/dot_general | solution.py:58
  75.4 0.0 reduce-scatter.5.cloned.1.call-update
  75.5 0.0 reduce-scatter.7.cloned.1.call-start
  75.5 0.0 copy-done.1
  75.5 7.1 %convolution_bitcast_fusion = f32[3584,256]{0,1:T(8,128)} fusion(bf16[1024,3584]{1,0:T(8,128)(2,1)} %bitcast.27, f32[1024,256]{1,0:T(8,128)S(1)} %copy-done.1, f32[1024]{0:T(1024)S(1)} %bitcast.29), kind=kOutput, calls=%fused_computation | convolution fusion | flops 1879572480 | bytes 12062720 | tf_op jit(solution)/shard_map/dot_general | solution.py:57
  82.6 5.1 %copy.23 = f32[3584,256]{1,0:T(8,128)} copy(f32[3584,256]{0,1:T(8,128)} %convolution_bitcast_fusion) | data formatting | bytes 7340032
  87.8 0.0 reduce-scatter.7.cloned.1.call-update
  87.8 0.1 copy.19
  87.9 20.5 %all-gather = f32[2,8,1]{0,2,1:T(1,128)S(1)} all-gather(f32[2,1,1]{0,2,1:T(1,128)S(1)} %copy.19), channel_id=2, replica_groups=mesh['dp'=8,'mp'=4] {'dp'}, dimensions={1}, use_global_device_ids=true | all-gather | bytes 72 | tf_op jit(solution)/shard_map/all_gather | solution.py:61
  108.4 0.1 copy.20
  108.5 0.7 fusion.3
  109.1 31.2 %reduce-scatter.5.cloned.1.call-done = f32[128,256]{0,1:T(8,128)} async-done(((f32[1024,256]{0,1:T(8,128)}), f32[128,256]{0,1:T(8,128)}) %reduce-scatter.5.cloned.1.call-update) | async-done | bytes 131088 | tf_op jit(solution)/shard_map/reduce_scatter | solution.py:60
  140.3 1.6 multiply_reduce_fusion.2
  141.9 82.4 %reduce-scatter.7.cloned.1.call-done = f32[448,256]{1,0:T(8,128)} async-done(((f32[3584,256]{1,0:T(8,128)}), f32[448,256]{1,0:T(8,128)}) %reduce-scatter.7.cloned.1.call-update) | async-done | bytes 458768
  224.3 1.2 copy.24
  225.5 0.7 multiply_reduce_fusion.1
  228.2 40.2 %psum.23 = f32[]{:T(128)} all-reduce(f32[]{:T(128)S(6)} %add.44), channel_id=1, replica_groups=mesh['dp'=8,'mp'=4] {'dp','mp'}, use_global_device_ids=true, to_apply=%region_10.11 | all-reduce | flops 1 | bytes 8 | tf_op jit(solution)/shard_map/psum | solution.py:66
  269.1 1.0 copy.21
  270.1 0.8 copy.22
  (20 shorter events, 0.1 us)
Async XLA Ops:
  7.2 6.9 %copy-start = (bf16[2,1,2,256,1024]{4,3,2,1,0:T(8,128)(2,1)S(1)}, bf16[2,1,2,256,1024]{4,3,2,1,0:T(8,128)(2,1)}, u32[]{:S(2)}) copy-start(bf16[2,1,2,256,1024]{4,3,2,1,0:T(8,128)(2,1)} %param.10) | copy-start | bytes 6291460
  7.2 62.9 %all-reduce.3.cloned.1.call-start = ((), (), s32[]{:S(2)}) async-start(), calls=%async_computation.4 | async-start | bytes 4194304 | tf_op jit(solution)/shard_map/psum | solution.py:36
  7.2 6.8 %copy-start.8 = (bf16[1024,256]{1,0:T(8,128)(2,1)S(1)}, bf16[1024,256]{1,0:T(8,128)(2,1)}, u32[]{:S(2)}) copy-start(bf16[1024,256]{1,0:T(8,128)(2,1)} %param.16) | copy-start | bytes 1572868
  15.7 56.1 %copy-start.3 = (f32[2,1,2,256]{3,2,1,0:T(2,128)S(1)}, f32[2,1,2,256]{3,2,1,0:T(2,128)}, u32[]{:S(2)}) copy-start(f32[2,1,2,256]{3,2,1,0:T(2,128)} %param.11) | copy-start | bytes 12292
  15.7 56.1 %copy-start.4 = (s32[2,1,2,256]{3,2,1,0:T(2,128)S(1)}, s32[2,1,2,256]{3,2,1,0:T(2,128)}, u32[]{:S(2)}) copy-start(s32[2,1,2,256]{3,2,1,0:T(2,128)} %param.12) | copy-start | bytes 12292
  15.7 56.1 %copy-start.5 = (s32[2,1,2]{2,1,0:T(1,128)S(1)}, s32[2,1,2]{2,1,0:T(1,128)}, u32[]{:S(2)}) copy-start(s32[2,1,2]{2,1,0:T(1,128)} %param.13) | copy-start | bytes 52
  15.7 56.5 %copy-start.7 = (f32[2]{0:T(128)S(1)}, f32[2]{0:T(128)}, u32[]{:S(2)}) copy-start(f32[2]{0:T(128)} %constant.51.clone) | copy-start | bytes 28
  15.8 124.5 %reduce-scatter.5.cloned.1.call-start = ((), (), s32[]{:S(2)}) async-start(), calls=%async_computation.2 | async-start | bytes 1179648 | tf_op jit(solution)/shard_map/reduce_scatter | solution.py:60
  72.3 3.2 %copy-start.1 = (f32[1024,256]{1,0:T(8,128)S(1)}, f32[1024,256]{1,0:T(8,128)}, u32[]{:S(2)}) copy-start(f32[1024,256]{1,0:T(8,128)} %get-tuple-element.19) | copy-start | bytes 3145732
  75.5 148.8 %reduce-scatter.7.cloned.1.call-start = ((), (), s32[]{:S(2)}) async-start(), calls=%async_computation.3 | async-start | bytes 4128768
  87.8 20.7 %copy-start.6 = (s32[2,8]{1,0:T(2,128)S(1)}, s32[2,8]{1,0:T(2,128)}, u32[]{:S(2)}) copy-start(s32[2,8]{1,0:T(2,128)} %param.14) | copy-start | bytes 196
  140.3 129.8 %copy-start.2 = (f32[128,256]{0,1:T(8,128)S(1)}, f32[128,256]{0,1:T(8,128)}, u32[]{:S(2)}) copy-start(f32[128,256]{0,1:T(8,128)} %reduce-scatter.5.cloned.1.call-done) | copy-start | bytes 393220
Sparse Core Ops, SparseCore 0:
  15.9 54.1 all-reduce.2
  75.6 64.6 reduce-scatter.4
  144.0 80.2 reduce-scatter.6

commit v2 on v1

v2 whole, which is shorter than its diff:
```python
import functools
import math

import jax
import jax.numpy as jnp
from jax import lax
from jax.experimental import pallas as pl
from jax.experimental.pallas import tpu as pltpu
from jax.sharding import PartitionSpec as P

TILE = 128
BETA = 0.1
CORES = 2
SIDES = 2
F32 = jnp.float32
MESH = pl.DeviceIdType.MESH
TRANSPOSED = (((0,), (0,)), ((), ()))


def remote(src, dst, send, recv, target):
    return pltpu.make_async_remote_copy(
        src_ref=src, dst_ref=dst, send_sem=send, recv_sem=recv, device_id=target, device_id_type=MESH
    )


def block_of(size):
    return next(width for width in (512, 256, 128, size) if size % width == 0)


def kernel(
    nd, nm, seq,
    hid_ref, rows_ref, ref_ref, live_ref, wa_ref, wb_ref,
    out_a, out_b, out_stats,
    hid, rows, wa, wb, parts, d2d_in, pair_sum, y_in, full, d_lat, d_read, raw_a, raw_b,
    xin_a, xin_b, zin_a, zin_b, margin_row, mine, mine_dp, stats_mp, stats_dp,
    load_w, load_h, load_r, d2d_s, d2d_r, y_s, y_r, g_s, g_r, x_s, x_r, z_s, z_r, m_s, m_r, p_s, p_r,
):
    tokens, rank = hid.shape[0], wa.shape[1]
    chunks = tokens // seq
    ny, nz = nm // CORES, nd // SIDES
    dp, mp = lax.axis_index("dp"), lax.axis_index("mp")
    core, y = mp % CORES, mp // CORES
    side, z = dp % SIDES, dp // SIDES
    ra, rb = out_a.shape[0], out_b.shape[0]
    root = math.sqrt(rank)

    def span(c):
        return pl.ds(c * seq, seq)

    loads = [
        pltpu.make_async_copy(wa_ref, wa, load_w.at[0]),
        pltpu.make_async_copy(wb_ref, wb, load_w.at[1]),
    ]
    load_hid = [pltpu.make_async_copy(hid_ref.at[span(c)], hid.at[span(c)], load_h.at[c]) for c in range(chunks)]
    load_rows = [pltpu.make_async_copy(rows_ref.at[span(c)], rows.at[span(c)], load_r.at[c]) for c in range(chunks)]
    loads[0].start()
    load_hid[0].start()
    loads[1].start()
    load_rows[0].start()
    for c in range(1, chunks):
        load_hid[c].start()
        load_rows[c].start()

    barrier = pltpu.get_barrier_semaphore()

    @pl.loop(1, nm)
    def _(k):
        pl.semaphore_signal(barrier, inc=1, device_id=(dp, (mp + k) % nm), device_id_type=MESH)

    @pl.loop(1, nd)
    def _(k):
        pl.semaphore_signal(barrier, inc=1, device_id=((dp + k) % nd, mp), device_id_type=MESH)

    pl.semaphore_wait(barrier, nm + nd - 2)

    partner = (dp, y * CORES + (1 - core))

    def d2d_copy(c):
        return remote(parts.at[1 - core, span(c)], d2d_in.at[span(c)], d2d_s.at[c], d2d_r.at[c], partner)

    def y_copy(k, c):
        target = (dp, ((y + k) % ny) * CORES + core)
        return remote(pair_sum.at[span(c)], y_in.at[ny - 1 - k, span(c)], y_s.at[k - 1, c], y_r.at[ny - 1 - k, c], target)

    def g_copy(c):
        return remote(full.at[core, span(c)], full.at[core, span(c)], g_s.at[c], g_r.at[c], partner)

    def g_arrival(c):
        here = full.at[1 - core, span(c)]
        return remote(here, here, g_s.at[c], g_r.at[c], partner)

    def forward(c):
        d2d_copy(c).wait_recv()
        pair_sum[span(c), :] = parts[core, span(c), :] + d2d_in[span(c), :]
        for k in range(1, ny):
            y_copy(k, c).start()

    for c in range(chunks):
        if c == 0:
            loads[0].wait()
        load_hid[c].wait()
        parts[0, span(c), :] = jnp.dot(hid[span(c), :], wa[...], preferred_element_type=F32)
        if c == 0:
            loads[1].wait()
        load_rows[c].wait()
        parts[1, span(c), :] = jnp.dot(rows[span(c), :], wb[...], preferred_element_type=F32)
        d2d_copy(c).start()
        if c:
            forward(c - 1)
    forward(chunks - 1)

    margin_row[...] = jnp.zeros_like(margin_row)
    lane = lax.broadcasted_iota(jnp.int32, margin_row.shape, 1)
    sign = jnp.where(lax.broadcasted_iota(jnp.int32, (2 * seq, 1), 0) < seq, 1.0, -1.0).astype(F32)

    def gradient(both, source, slopes, total, first):
        width = block_of(total.shape[0])

        @pl.loop(0, total.shape[0] // width)
        def _(j):
            at = pl.ds(pl.multiple_of(j * width, width), width)
            term = lax.dot_general(source[both, at], slopes[both, :], TRANSPOSED, preferred_element_type=F32)
            total[at, :] = term if first else total[at, :] + term

    for p in range(chunks // 2):
        for c in (2 * p, 2 * p + 1):
            value = pair_sum[span(c), :]
            for k in range(ny - 1, 0, -1):
                y_copy(k, c).wait_recv()
                value = value + y_in[ny - 1 - k, span(c), :]
            full[core, span(c), :] = value
            g_copy(c).start()
        for c in (2 * p, 2 * p + 1):
            g_arrival(c).wait_recv()
        both = pl.ds(2 * p * seq, 2 * seq)
        latent, readout = full[0, both, :], full[1, both, :]
        shift = jnp.sum(latent * readout, axis=1, keepdims=True) / root
        chance = jnp.exp(ref_ref[both, :])
        denom = 1.0 - chance + chance * jnp.exp(shift)
        gain = shift - jnp.log(denom)
        live = live_ref[both, :]
        margin = BETA * jnp.sum(live * gain * sign, axis=0, keepdims=True)
        slope = -jax.nn.sigmoid(-margin)
        factor = live * (slope * BETA) * sign * (1.0 - chance) / denom / root
        d_lat[both, :] = (factor * readout).astype(jnp.bfloat16)
        d_read[both, :] = (factor * latent).astype(jnp.bfloat16)
        margin_row[...] = jnp.where(lane == p + 1, margin, margin_row[...])
        gradient(both, hid, d_lat, raw_a, p == 0)
        gradient(both, rows, d_read, raw_b, p == 0)

    def at_a(d):
        return pl.ds(pl.multiple_of(d * ra, 8), ra)

    def at_b(d):
        return pl.ds(pl.multiple_of(d * rb, 8), rb)

    def x_copies(k):
        to = (z + 1 + k) % nz
        d = to * SIDES + (1 - side)
        target = (z * SIDES + (1 - side), mp)
        return (
            remote(raw_a.at[at_a(d)], xin_a.at[k], x_s.at[k, 0], x_r.at[k, 0], target),
            remote(raw_b.at[at_b(d)], xin_b.at[k], x_s.at[k, 1], x_r.at[k, 1], target),
        )

    def z_copies(k):
        to = (z + 1 + k) % nz
        target = (to * SIDES + side, mp)
        return (
            remote(xin_a.at[k], zin_a.at[k], z_s.at[k, 0], z_r.at[k, 0], target),
            remote(xin_b.at[k], zin_b.at[k], z_s.at[k, 1], z_r.at[k, 1], target),
        )

    @pl.loop(0, nz)
    def _(k):
        for copy in x_copies(k):
            copy.start()

    @pl.loop(0, nz - 1)
    def _(k):
        d = ((z + 1 + k) % nz) * SIDES + side
        over_a, over_b = x_copies(k)
        on_a, on_b = z_copies(k)
        over_a.wait_recv()
        xin_a[k, :, :] = xin_a[k, :, :] + raw_a[at_a(d), :]
        on_a.start()
        over_b.wait_recv()
        xin_b[k, :, :] = xin_b[k, :, :] + raw_b[at_b(d), :]
        on_b.start()

    over_a, over_b = x_copies(nz - 1)
    over_a.wait_recv()
    out_a[...] = xin_a[nz - 1, :, :] + raw_a[at_a(dp), :]
    over_b.wait_recv()
    out_b[...] = xin_b[nz - 1, :, :] + raw_b[at_b(dp), :]

    @pl.loop(0, nz - 1)
    def _(k):
        on_a, on_b = z_copies(k)
        on_a.wait_recv()
        out_a[...] += zin_a[k, :, :]
        on_b.wait_recv()
        out_b[...] += zin_b[k, :, :]

    def total_of(value):
        return jnp.sum(jnp.sum(value * value, axis=0, keepdims=True), axis=1, keepdims=True)

    mine[0, :, :] = jnp.where(lane == 0, total_of(out_a[...]) + total_of(out_b[...]), margin_row[...])

    def m_copy(k):
        return remote(mine.at[0], stats_mp.at[mp], m_s.at[k - 1], m_r.at[k - 1], (dp, (mp + k) % nm))

    def p_copy(k):
        return remote(mine_dp.at[0], stats_dp.at[dp], p_s.at[k - 1], p_r.at[k - 1], ((dp + k) % nd, mp))

    @pl.loop(1, nm)
    def _(k):
        m_copy(k).start()

    stats_mp[mp, :, :] = mine[0, :, :]

    @pl.loop(1, nm)
    def _(k):
        m_copy(k).wait_recv()

    squares = stats_mp[0, :, :]
    for k in range(1, nm):
        squares = squares + stats_mp[k, :, :]
    mine_dp[0, :, :] = jnp.where(lane == 0, squares, stats_mp[0, :, :])

    @pl.loop(1, nd)
    def _(k):
        p_copy(k).start()

    stats_dp[dp, :, :] = mine_dp[0, :, :]

    @pl.loop(1, nd)
    def _(k):
        p_copy(k).wait_recv()

    out_stats[...] = stats_dp[...]

    for c in range(chunks):
        d2d_copy(c).wait_send()
        g_copy(c).wait_send()
        for k in range(1, ny):
            y_copy(k, c).wait_send()

    @pl.loop(0, nz)
    def _(k):
        for copy in x_copies(k):
            copy.wait_send()

    @pl.loop(0, nz - 1)
    def _(k):
        for copy in z_copies(k):
            copy.wait_send()

    @pl.loop(1, nm)
    def _(k):
        m_copy(k).wait_send()

    @pl.loop(1, nd)
    def _(k):
        p_copy(k).wait_send()


def per_device(
    nd, nm,
    hidden_activation,
    target_head_rows,
    reference_log_probability,
    response_token_mask,
    sequence_tile_lengths,
    pair_destination,
    adapter_down_first,
    adapter_down_second,
):
    micro_count, pairs_dev, _, seq, ff = hidden_activation.shape
    width = target_head_rows.shape[-1]
    rank = adapter_down_first.shape[1]
    tokens = micro_count * pairs_dev * 2 * seq
    chunks = tokens // seq
    ny, nz = nm // CORES, nd // SIDES
    ra, rb = ff // nd, width // nd
    positions = jnp.arange(seq) // TILE
    live = ((response_token_mask == 1) & (positions < sequence_tile_lengths[..., None])).astype(F32)
    vmem = pl.BlockSpec(memory_space=pltpu.VMEM)
    hbm = pl.BlockSpec(memory_space=pl.ANY)
    V = pltpu.VMEM
    dma = pltpu.SemaphoreType.DMA
    bf16 = jnp.bfloat16
    raw_a, raw_b, stats = pl.pallas_call(
        functools.partial(kernel, nd, nm, seq),
        out_shape=(
            jax.ShapeDtypeStruct((ra, rank), F32),
            jax.ShapeDtypeStruct((rb, rank), F32),
            jax.ShapeDtypeStruct((nd, 1, 128), F32),
        ),
        in_specs=[hbm, hbm, vmem, vmem, hbm, hbm],
        out_specs=(vmem, vmem, vmem),
        scratch_shapes=[
            V((tokens, ff), bf16), V((tokens, width), bf16), V((ff, rank), bf16), V((width, rank), bf16),
            V((2, tokens, rank), F32), V((tokens, rank), F32), V((tokens, rank), F32),
            V((ny - 1, tokens, rank), F32), V((2, tokens, rank), F32),
            V((tokens, rank), bf16), V((tokens, rank), bf16), V((ff, rank), F32), V((width, rank), F32),
            V((nz, ra, rank), F32), V((nz, rb, rank), F32), V((nz - 1, ra, rank), F32), V((nz - 1, rb, rank), F32),
            V((1, 128), F32), V((1, 1, 128), F32), V((1, 1, 128), F32), V((nm, 1, 128), F32), V((nd, 1, 128), F32),
            dma((2,)), dma((chunks,)), dma((chunks,)), dma((chunks,)), dma((chunks,)),
            dma((ny - 1, chunks)), dma((ny - 1, chunks)), dma((chunks,)), dma((chunks,)),
            dma((nz, 2)), dma((nz, 2)), dma((nz - 1, 2)), dma((nz - 1, 2)),
            dma((nm - 1,)), dma((nm - 1,)), dma((nd - 1,)), dma((nd - 1,)),
        ],
        compiler_params=pltpu.CompilerParams(collective_id=0, has_side_effects=True, vmem_limit_bytes=60 * 2**20),
    )(
        hidden_activation.reshape(tokens, ff),
        target_head_rows.reshape(tokens, width),
        reference_log_probability.reshape(tokens, 1),
        live.reshape(tokens, 1),
        adapter_down_first,
        adapter_down_second,
    )
    stats = stats[:, 0, :]
    pairs = micro_count * pairs_dev
    all_margins = (
        stats[:, 1 : 1 + pairs].reshape(nd, micro_count, pairs_dev).transpose(1, 0, 2).reshape(micro_count, -1)
    )
    targets = lax.axis_index("dp") * pairs_dev + jnp.arange(pairs_dev)
    hits = pair_destination[:, :, None] == targets[None, None, :]
    pair_margin = jnp.sum(jnp.where(hits, all_margins[:, :, None], 0.0), axis=1)
    mean_loss = jnp.mean(jax.nn.softplus(-all_margins))
    scale = 1.0 / jnp.sqrt(jnp.sum(stats[:, 0]) / ((ff + width) * nm * rank) + 1e-06)
    return (pair_margin, mean_loss, raw_a * scale, raw_b * scale)


def solution(mesh):
    in_specs = (
        P(None, "dp", None, None, "mp"),
        P(None, "dp", None, None, "mp"),
        P(None, "dp", None, None),
        P(None, "dp", None, None),
        P(None, "dp", None),
        P(),
        P("mp", None),
        P("mp", None),
    )
    out_specs = (P(None, "dp"), P(), P(("mp", "dp"), None), P(("mp", "dp"), None))
    return jax.shard_map(
        functools.partial(per_device, mesh.shape["dp"], mesh.shape["mp"]),
        mesh=mesh, in_specs=in_specs, out_specs=out_specs, check_vma=False,
    )
```

time: 279 us -> 126 us (0.45)
  waiting for transfers between devices: 168 us -> 0 us
  Pallas kernels: 0 us -> 112 us
  blocking collectives: 60.7 us -> 0 us
  matrix products: 18.7 us -> 0 us
  between operations: 17.6 us -> 3.12 us
  local copies, waits for them, and re-layouts: 8.3 us -> 3.81 us
    pallas_call x0 -> x1, Pallas kernels: none -> 112 us  [per_device(): pl.pallas_call(functools.partial(kernel, nd, nm, seq), out_shape=(jax.Sha...]
    unnamed x4 -> x0, waiting for transfers between devices: 82.4 us -> none
    psum x1 -> x0, waiting for transfers between devices: 54.2 us -> none  [per_device(): latent, readout = lax.psum((latent, readout), 'mp')]
    psum x1 -> x0, blocking collectives: 40.2 us -> none  [per_device(): lax.psum(jnp.sum(shard_a * shard_a) + jnp.sum(shard_b * shard_b), ('dp',...]
    reduce_scatter x1 -> x0, waiting for transfers between devices: 31.2 us -> none  [per_device(): shard_b = lax.psum_scatter(raw_b, 'dp', scatter_dimension=0, tiled=True)]
    all_gather x1 -> x0, blocking collectives: 20.5 us -> none  [per_device(): all_margins = lax.all_gather(margins, 'dp', axis=1, tiled=True)]
    dot_general x4 -> x0, matrix products: 18.7 us -> none  [the longest x1 7.1 us: per_device(): lax.dot_general(hidden, d_latent, contract, preferred_element_type=jnp.fl...]
    unnamed x23 -> x2, local copies, waits for them, and re-layouts: 8.11 us -> 0.01 us
  transfers between devices with their start and end apart: 3 -> 0, of which waited for: 3 -> 0; matrix products, arithmetic and copies ran while one was open for 5% -> 0% of each run, Pallas kernels for 0% -> 0%
where the time goes in v2:
time: 126 us
  Pallas kernels  112 us (89%)
  other arithmetic  6.69 us (5%)
  local copies, waits for them, and re-layouts  3.81 us (3%)
  between operations  3.12 us (2%)
    pallas_call x1, Pallas kernels, per_device(): pl.pallas_call(functools.partial(kernel, nd, nm, seq), out_shape=(jax.Sha...  112 us
    mul x2, other arithmetic, per_device(): return (pair_margin, mean_loss, raw_a * scale, raw_b * scale)  3.39 us

profile of v2, /device:TPU:0, one launch (start us, length us, event | category | flops | bytes accessed | tf_op | source)
XLA Modules:
  0.0 125.7 jit_solution(8072669537786137365)
XLA Ops:
  0.6 0.8 and_convert_fusion
  1.4 1.2 reshape.63.live_ref
  2.6 1.8 %reshape.62.ref_ref = f32[1024,1]{1,0:T(8,128)} reshape(f32[2,1,2,256]{3,2,1,0:T(2,128)} %param.10) | data formatting | bytes 8192 | tf_op jit(solution)/shard_map/reshape | solution.py:318
  4.4 0.0 copy-start
  4.4 112.1 %shard_map.111 = (f32[448,256]{1,0:T(8,128)}, f32[128,256]{1,0:T(8,128)}, f32[8,1,128]{2,1,0:T(1,128)}) custom-call(bf16[1024,3584]{1,0:T(8,128)(2,1)} %bitcast.32, bf16[1024,1024]{1,0:T(8,128)(2,1)} %bitcast.33, f32[1024,1]{1,0:T(8,128)} %reshape.62.ref_ref, f32[1024,1]{1,0:T(8,128)} %reshape.63.live_ref, bf16[3584,256]{1,0:T(8,128)(2,1)} %wa_ref.1, ...), custom_call_target="tpu_custom_call" | custom-call | tf_op jit(solution)/shard_map/pallas_call | solution.py:293
  116.5 1.3 %slice_reduce_fusion = f32[]{:T(128)} fusion(f32[8,128]{1,0:T(8,128)} %bitcast.34), kind=kLoop, calls=%fused_computation.3 | loop fusion | flops 7 | bytes 36 | tf_op jit(solution)/shard_map/reduce_sum | solution.py:332
  118.5 1.6 %broadcast_multiply_fusion.1 = f32[128,256]{1,0:T(8,128)} fusion(f32[128,256]{1,0:T(8,128)} %get-tuple-element.9, f32[]{:T(128)S(6)} %sqrt.3), kind=kLoop, calls=%fused_computation.1 | loop fusion | flops 32768 | bytes 262148 | tf_op jit(solution)/shard_map/mul | solution.py:333
  120.1 1.8 %broadcast_multiply_fusion = f32[448,256]{1,0:T(8,128)} fusion(f32[448,256]{1,0:T(8,128)} %get-tuple-element.8, f32[]{:T(128)S(6)} %sqrt.3), kind=kLoop, calls=%fused_computation | loop fusion | flops 114688 | bytes 917508 | tf_op jit(solution)/shard_map/mul | solution.py:333
  121.9 0.7 slice.6
  122.6 0.1 copy.15
  122.7 0.0 copy-done
  122.7 0.6 fusion
  123.3 0.6 fusion.1
  (1 shorter events, 0.0 us)
Async XLA Ops:
  4.4 118.3 %copy-start = (s32[2,8]{1,0:T(2,128)S(1)}, s32[2,8]{1,0:T(2,128)}, u32[]{:S(2)}) copy-start(s32[2,8]{1,0:T(2,128)} %param.13) | copy-start | bytes 196

commit v3 on v2

--- a/solution.py
+++ b/solution.py
@@ -29,11 +29,11 @@
 
 def kernel(
     nd, nm, seq,
-    hid_ref, rows_ref, ref_ref, live_ref, wa_ref, wb_ref,
+    hid_ref, rows_ref, token_ref, wa_ref, wb_ref,
     out_a, out_b, out_stats,
     hid, rows, wa, wb, parts, d2d_in, pair_sum, y_in, full, d_lat, d_read, raw_a, raw_b,
-    xin_a, xin_b, zin_a, zin_b, margin_row, mine, mine_dp, stats_mp, stats_dp,
-    load_w, load_h, load_r, d2d_s, d2d_r, y_s, y_r, g_s, g_r, x_s, x_r, z_s, z_r, m_s, m_r, p_s, p_r,
+    xin_a, xin_b, lin_a, lin_b, rin_a, rin_b, ref_col, live_col, margin_row, mine, mine_dp, stats_mp, stats_dp,
+    load_w, load_h, load_r, d2d_s, d2d_r, y_s, y_r, g_s, g_r, x_s, x_r, z_s, l_r, r_r, m_s, m_r, p_s, p_r,
 ):
     tokens, rank = hid.shape[0], wa.shape[1]
     chunks = tokens // seq
@@ -61,6 +61,12 @@
         load_hid[c].start()
         load_rows[c].start()
 
+    columns = jnp.transpose(token_ref[...])
+    place = lax.broadcasted_iota(jnp.int32, columns.shape, 1)
+    for c in range(chunks):
+        ref_col[span(c), :] = jnp.sum(jnp.where(place == c, columns, 0.0), axis=1, keepdims=True)
+        live_col[span(c), :] = jnp.sum(jnp.where(place == chunks + c, columns, 0.0), axis=1, keepdims=True)
+
     barrier = pltpu.get_barrier_semaphore()
 
     @pl.loop(1, nm)
@@ -122,6 +128,38 @@
             term = lax.dot_general(source[both, at], slopes[both, :], TRANSPOSED, preferred_element_type=F32)
             total[at, :] = term if first else total[at, :] + term
 
+    def at(d, which):
+        size = rb if which else ra
+        return pl.ds(pl.multiple_of(d * size, 8), size)
+
+    def order(k):
+        high = (2 * z) // nz
+        low_z = z + high * (nz - 1 - 2 * z)
+        d = nz - 1 - k - (k + low_z) // max(nz - 1, 1)
+        return d + high * (nz - 1 - 2 * d)
+
+    def x_copy(k, d, which):
+        raw, xin = (raw_b, xin_b) if which else (raw_a, xin_a)
+        source = raw.at[at(d * SIDES + (1 - side), which)]
+        return remote(source, xin.at[k], x_s.at[k, which], x_r.at[k, which], (z * SIDES + (1 - side), mp))
+
+    def l_copy(k, d, which):
+        xin, lin = (xin_b, lin_b) if which else (xin_a, lin_a)
+        target = (((z + 1) % nz) * SIDES + side, mp)
+        return remote(xin.at[k], lin.at[d], z_s.at[k, which], l_r.at[d, which], target)
+
+    def r_copy(k, d, which):
+        xin, rin = (xin_b, rin_b) if which else (xin_a, rin_a)
+        target = (((z + nz - 1) % nz) * SIDES + side, mp)
+        return remote(xin.at[k], rin.at[d], z_s.at[k, which], r_r.at[d, which], target)
+
+    def start_x(which):
+        @pl.loop(0, nz - 1)
+        def _(k):
+            x_copy(k, order(k), which).start()
+
+        x_copy(nz - 1, z, which).start()
+
     for p in range(chunks // 2):
         for c in (2 * p, 2 * p + 1):
             value = pair_sum[span(c), :]
@@ -135,72 +173,65 @@
         both = pl.ds(2 * p * seq, 2 * seq)
         latent, readout = full[0, both, :], full[1, both, :]
         shift = jnp.sum(latent * readout, axis=1, keepdims=True) / root
-        chance = jnp.exp(ref_ref[both, :])
+        chance = jnp.exp(ref_col[both, :])
         denom = 1.0 - chance + chance * jnp.exp(shift)
         gain = shift - jnp.log(denom)
-        live = live_ref[both, :]
+        live = live_col[both, :]
         margin = BETA * jnp.sum(live * gain * sign, axis=0, keepdims=True)
         slope = -jax.nn.sigmoid(-margin)
         factor = live * (slope * BETA) * sign * (1.0 - chance) / denom / root
         d_lat[both, :] = (factor * readout).astype(jnp.bfloat16)
         d_read[both, :] = (factor * latent).astype(jnp.bfloat16)
         margin_row[...] = jnp.where(lane == p + 1, margin, margin_row[...])
+        gradient(both, rows, d_read, raw_b, p == 0)
+        if p == chunks // 2 - 1:
+            start_x(1)
         gradient(both, hid, d_lat, raw_a, p == 0)
-        gradient(both, rows, d_read, raw_b, p == 0)
-
-    def at_a(d):
-        return pl.ds(pl.multiple_of(d * ra, 8), ra)
-
-    def at_b(d):
-        return pl.ds(pl.multiple_of(d * rb, 8), rb)
-
-    def x_copies(k):
-        to = (z + 1 + k) % nz
-        d = to * SIDES + (1 - side)
-        target = (z * SIDES + (1 - side), mp)
-        return (
-            remote(raw_a.at[at_a(d)], xin_a.at[k], x_s.at[k, 0], x_r.at[k, 0], target),
-            remote(raw_b.at[at_b(d)], xin_b.at[k], x_s.at[k, 1], x_r.at[k, 1], target),
+    start_x(0)
+
+    for which in (1, 0):
+        raw, xin, lin, rin = (raw_a, xin_a, lin_a, rin_a) if which == 0 else (raw_b, xin_b, lin_b, rin_b)
+
+        @pl.loop(0, nz - 1)
+        def _(k):
+            d = order(k)
+            x_copy(k, d, which).wait_recv()
+            xin[k, :, :] = xin[k, :, :] + raw[at(d * SIDES + side, which), :]
+
+            @pl.when(d > z)
+            def _():
+                @pl.when(z > 0)
+                def _():
+                    l_copy(k, d, which).wait_recv()
+                    xin[k, :, :] = xin[k, :, :] + lin[d, :, :]
+
+                l_copy(k, d, which).start()
+
+            @pl.when(d < z)
+            def _():
+                @pl.when(z < nz - 1)
+                def _():
+                    r_copy(k, d, which).wait_recv()
+                    xin[k, :, :] = xin[k, :, :] + rin[d, :, :]
+
+                r_copy(k, d, which).start()
+
+    for which in (1, 0):
+        raw, xin, lin, rin, out = (
+            (raw_a, xin_a, lin_a, rin_a, out_a) if which == 0 else (raw_b, xin_b, lin_b, rin_b, out_b)
         )
-
-    def z_copies(k):
-        to = (z + 1 + k) % nz
-        target = (to * SIDES + side, mp)
-        return (
-            remote(xin_a.at[k], zin_a.at[k], z_s.at[k, 0], z_r.at[k, 0], target),
-            remote(xin_b.at[k], zin_b.at[k], z_s.at[k, 1], z_r.at[k, 1], target),
-        )
-
-    @pl.loop(0, nz)
-    def _(k):
-        for copy in x_copies(k):
-            copy.start()
-
-    @pl.loop(0, nz - 1)
-    def _(k):
-        d = ((z + 1 + k) % nz) * SIDES + side
-        over_a, over_b = x_copies(k)
-        on_a, on_b = z_copies(k)
-        over_a.wait_recv()
-        xin_a[k, :, :] = xin_a[k, :, :] + raw_a[at_a(d), :]
-        on_a.start()
-        over_b.wait_recv()
-        xin_b[k, :, :] = xin_b[k, :, :] + raw_b[at_b(d), :]
-        on_b.start()
-
-    over_a, over_b = x_copies(nz - 1)
-    over_a.wait_recv()
-    out_a[...] = xin_a[nz - 1, :, :] + raw_a[at_a(dp), :]
-    over_b.wait_recv()
-    out_b[...] = xin_b[nz - 1, :, :] + raw_b[at_b(dp), :]
-
-    @pl.loop(0, nz - 1)
-    def _(k):
-        on_a, on_b = z_copies(k)
-        on_a.wait_recv()
-        out_a[...] += zin_a[k, :, :]
-        on_b.wait_recv()
-        out_b[...] += zin_b[k, :, :]
+        x_copy(nz - 1, z, which).wait_recv()
+        out[...] = xin[nz - 1, :, :] + raw[at(dp, which), :]
+
+        @pl.when(z > 0)
+        def _():
+            l_copy(0, z, which).wait_recv()
+            out[...] += lin[z, :, :]
+
+        @pl.when(z < nz - 1)
+        def _():
+            r_copy(0, z, which).wait_recv()
+            out[...] += rin[z, :, :]
 
     def total_of(value):
         return jnp.sum(jnp.sum(value * value, axis=0, keepdims=True), axis=1, keepdims=True)
@@ -239,6 +270,14 @@
         p_copy(k).wait_recv()
 
     out_stats[...] = stats_dp[...]
+    squared = stats_dp[0, :, :]
+    for k in range(1, nd):
+        squared = squared + stats_dp[k, :, :]
+    squared = jnp.sum(jnp.where(lane == 0, squared, 0.0), axis=1, keepdims=True)
+    count = (raw_a.shape[0] + raw_b.shape[0]) * nm * rank
+    scale = 1.0 / jnp.sqrt(squared / count + 1e-06)
+    out_a[...] = out_a[...] * scale
+    out_b[...] = out_b[...] * scale
 
     for c in range(chunks):
         d2d_copy(c).wait_send()
@@ -246,15 +285,15 @@
         for k in range(1, ny):
             y_copy(k, c).wait_send()
 
-    @pl.loop(0, nz)
-    def _(k):
-        for copy in x_copies(k):
-            copy.wait_send()
-
-    @pl.loop(0, nz - 1)
-    def _(k):
-        for copy in z_copies(k):
-            copy.wait_send()
+    for which in (1, 0):
+
+        @pl.loop(0, nz)
+        def _(k):
+            x_copy(k, z, which).wait_send()
+
+        @pl.loop(0, nz - 1)
+        def _(k):
+            l_copy(k, z, which).wait_send()
 
     @pl.loop(1, nm)
     def _(k):
@@ -290,33 +329,33 @@
     V = pltpu.VMEM
     dma = pltpu.SemaphoreType.DMA
     bf16 = jnp.bfloat16
-    raw_a, raw_b, stats = pl.pallas_call(
+    grad_a, grad_b, stats = pl.pallas_call(
         functools.partial(kernel, nd, nm, seq),
         out_shape=(
             jax.ShapeDtypeStruct((ra, rank), F32),
             jax.ShapeDtypeStruct((rb, rank), F32),
             jax.ShapeDtypeStruct((nd, 1, 128), F32),
         ),
-        in_specs=[hbm, hbm, vmem, vmem, hbm, hbm],
+        in_specs=[hbm, hbm, vmem, hbm, hbm],
         out_specs=(vmem, vmem, vmem),
         scratch_shapes=[
             V((tokens, ff), bf16), V((tokens, width), bf16), V((ff, rank), bf16), V((width, rank), bf16),
             V((2, tokens, rank), F32), V((tokens, rank), F32), V((tokens, rank), F32),
             V((ny - 1, tokens, rank), F32), V((2, tokens, rank), F32),
             V((tokens, rank), bf16), V((tokens, rank), bf16), V((ff, rank), F32), V((width, rank), F32),
-            V((nz, ra, rank), F32), V((nz, rb, rank), F32), V((nz - 1, ra, rank), F32), V((nz - 1, rb, rank), F32),
+            V((nz, ra, rank), F32), V((nz, rb, rank), F32), V((nz, ra, rank), F32), V((nz, rb, rank), F32),
+            V((nz, ra, rank), F32), V((nz, rb, rank), F32), V((tokens, 1), F32), V((tokens, 1), F32),
             V((1, 128), F32), V((1, 1, 128), F32), V((1, 1, 128), F32), V((nm, 1, 128), F32), V((nd, 1, 128), F32),
             dma((2,)), dma((chunks,)), dma((chunks,)), dma((chunks,)), dma((chunks,)),
             dma((ny - 1, chunks)), dma((ny - 1, chunks)), dma((chunks,)), dma((chunks,)),
-            dma((nz, 2)), dma((nz, 2)), dma((nz - 1, 2)), dma((nz - 1, 2)),
+            dma((nz, 2)), dma((nz, 2)), dma((nz - 1, 2)), dma((nz, 2)), dma((nz, 2)),
             dma((nm - 1,)), dma((nm - 1,)), dma((nd - 1,)), dma((nd - 1,)),
         ],
         compiler_params=pltpu.CompilerParams(collective_id=0, has_side_effects=True, vmem_limit_bytes=60 * 2**20),
     )(
         hidden_activation.reshape(tokens, ff),
         target_head_rows.reshape(tokens, width),
-        reference_log_probability.reshape(tokens, 1),
-        live.reshape(tokens, 1),
+        jnp.concatenate([reference_log_probability.reshape(chunks, seq), live.reshape(chunks, seq)]),
         adapter_down_first,
         adapter_down_second,
     )
@@ -329,8 +368,7 @@
     hits = pair_destination[:, :, None] == targets[None, None, :]
     pair_margin = jnp.sum(jnp.where(hits, all_margins[:, :, None], 0.0), axis=1)
     mean_loss = jnp.mean(jax.nn.softplus(-all_margins))
-    scale = 1.0 / jnp.sqrt(jnp.sum(stats[:, 0]) / ((ff + width) * nm * rank) + 1e-06)
-    return (pair_margin, mean_loss, raw_a * scale, raw_b * scale)
+    return (pair_margin, mean_loss, grad_a, grad_b)
 
 
 def solution(mesh):

time: 126 us -> 114 us (0.905)
  Pallas kernels: 112 us -> 104 us
  other arithmetic: 6.69 us -> 2.63 us
    pallas_call x1, Pallas kernels: 112 us -> 104 us  [per_device(): pl.pallas_call(functools.partial(kernel, nd, nm, seq), out_shape=(jax.Sha...]
    mul x2 -> x0, other arithmetic: 3.39 us -> none  [per_device(): return (pair_margin, mean_loss, raw_a * scale, raw_b * scale)]
    unnamed x2 -> x4, local copies, waits for them, and re-layouts: 0.01 us -> 3.38 us
    reshape x2, local copies, waits for them, and re-layouts: 2.98 us -> 0.72 us  [the longest x1 0.7 us: per_device(): reference_log_probability.reshape(chunks, seq)]
    reduce_sum x1 -> x0, other arithmetic: 1.28 us -> none  [per_device(): jnp.sum(stats[:, 0]) / ((ff + width) * nm * rank) + 1e-06]
where the time goes in v3:
time: 114 us
  Pallas kernels  104 us (91%)
  local copies, waits for them, and re-layouts  4.94 us (4%)
  other arithmetic  2.63 us (2%)
  between operations  2.44 us (2%)
    pallas_call x1, Pallas kernels, per_device(): pl.pallas_call(functools.partial(kernel, nd, nm, seq), out_shape=(jax.Sha...  104 us
    unnamed x4, local copies, waits for them, and re-layouts  3.38 us

profile of v3, /device:TPU:0, one launch (start us, length us, event | category | flops | bytes accessed | tf_op | source)
XLA Modules:
  0.0 114.0 jit_solution(9283715912868470741)
XLA Ops:
  0.6 0.8 and_convert_fusion
  1.4 0.7 reshape.57
  2.1 0.6 pad_maximum_fusion.token_ref
  2.7 0.0 copy-start
  2.7 104.0 %shard_map.111 = (f32[448,256]{1,0:T(8,128)}, f32[128,256]{1,0:T(8,128)}, f32[8,1,128]{2,1,0:T(1,128)}) custom-call(bf16[1024,3584]{1,0:T(8,128)(2,1)} %bitcast.32, bf16[1024,1024]{1,0:T(8,128)(2,1)} %bitcast.33, f32[8,256]{1,0:T(8,128)} %pad_maximum_fusion.token_ref, bf16[3584,256]{1,0:T(8,128)(2,1)} %wa_ref.1, bf16[1024,256]{1,0:T(8,128)(2,1)} %wb_ref.1), custom_call_target="tpu_custom_call" | custom-call | tf_op jit(solution)/shard_map/pallas_call | solution.py:332
  106.7 0.8 slice.3
  107.5 0.1 copy.12
  107.6 0.6 fusion.1
  108.8 0.0 copy-done
  108.9 0.6 fusion
  109.5 1.8 %copy.15 = f32[448,256]{1,0:T(8,128)} copy(f32[448,256]{1,0:T(8,128)} %get-tuple-element.16) | data formatting | bytes 917504
  111.3 1.6 %copy.16 = f32[128,256]{1,0:T(8,128)} copy(f32[128,256]{1,0:T(8,128)} %get-tuple-element.17) | data formatting | bytes 262144
  (2 shorter events, 0.0 us)
Async XLA Ops:
  2.7 106.1 %copy-start = (s32[2,8]{1,0:T(2,128)S(1)}, s32[2,8]{1,0:T(2,128)}, u32[]{:S(2)}) copy-start(s32[2,8]{1,0:T(2,128)} %param.13) | copy-start | bytes 196
